TPU v7x, 32 devices: a whole 2x2x4 slice. The times are simulated.
32 devices in a mesh: mpo: 4 (over y, x), sec: 8 (over z, core).
Axes of the slice: x: 2, y: 2, z: 4, core: 2. Of those that a mesh axis runs over, the one named last changes fastest.
Arguments:
- wavefunction: bfloat16 [8, 256, 256], P('sec'), may hold values from -6 to 6
- left_dims: int32 [8], P('sec'), may hold values from 64 to 256
- right_dims: int32 [8], P('sec'), may hold values from 64 to 256
- left_environment_block: bfloat16 [1280, 256, 256], P(('mpo', 'sec')), may hold values from -0.375 to 0.375
- right_env: bfloat16 [1280, 256, 256], P(('mpo', 'sec')), may hold values from -0.03125 to 0.03125
- task_out: int32 [1280], P(('mpo', 'sec')), may hold values from 0 to 7
- task_in: int32 [1280], P(('mpo', 'sec')), may hold values from 0 to 7
Outputs:
- applied: bfloat16 [8, 256, 256], P('sec', 'mpo')
All inputs are finite; a program needn't handle non-finite values.
Results may differ from a plain program's by a relative error of at most 0.0078.
Values may be sent and summed in bfloat16 or wider, within the bound.
A program may use at most 128 MiB of HBM per device.

v0:
```python
import jax
import jax.numpy as jnp
from jax import lax
from jax.sharding import PartitionSpec as P


def on_device(
    wavefunction, left_dims, right_dims, left_environment_block, right_env, task_out, task_in
):
    block_rows = wavefunction.shape[1]
    block_cols = wavefunction.shape[2]
    groups = lax.axis_size("mpo")
    quarter = block_rows // groups
    row_ids = lax.broadcasted_iota(jnp.int32, wavefunction.shape, 1)
    col_ids = lax.broadcasted_iota(jnp.int32, wavefunction.shape, 2)
    live_cells = (row_ids < left_dims[:, None, None]) & (col_ids < right_dims[:, None, None])
    masked = jnp.where(live_cells, wavefunction, jnp.zeros_like(wavefunction))
    blocks = lax.all_gather(masked, "sec", axis=0, tiled=True)
    sectors = blocks.shape[0]
    number_of_tasks = task_out.shape[0]
    picked_tasks = jnp.take(blocks, task_in, axis=0)
    middle_tensor = jnp.einsum(
        "xvz,xzy->xvy", left_environment_block, picked_tasks, preferred_element_type=jnp.float32
    ).astype(jnp.bfloat16)
    middle_split = middle_tensor.reshape(number_of_tasks, groups, quarter, block_cols)
    task_product = jnp.einsum(
        "tmrc,tdc->mtrd", middle_split, right_env, preferred_element_type=jnp.float32
    )

    def sector_sums(terms):
        return jax.ops.segment_sum(terms, task_out, num_segments=sectors)

    summed = jax.vmap(sector_sums)(task_product)
    row_sums = lax.psum_scatter(summed, "mpo", scatter_dimension=0, tiled=True)
    own_sum = lax.psum_scatter(row_sums[0], "sec", scatter_dimension=0, tiled=True)
    out_rows = (
        lax.broadcasted_iota(jnp.int32, (1, quarter, block_cols), 1)
        + lax.axis_index("mpo") * quarter
    )
    out_cols = lax.broadcasted_iota(jnp.int32, (1, quarter, block_cols), 2)
    kept_cells = (out_rows < left_dims[:, None, None]) & (out_cols < right_dims[:, None, None])
    return jnp.where(kept_cells, own_sum, jnp.zeros_like(own_sum)).astype(jnp.bfloat16)


def solution(mesh):
    return jax.shard_map(
        on_device,
        mesh=mesh,
        in_specs=(
            P("sec", None, None),
            P("sec"),
            P("sec"),
            P(("mpo", "sec"), None, None),
            P(("mpo", "sec"), None, None),
            P(("mpo", "sec")),
            P(("mpo", "sec")),
        ),
        out_specs=P("sec", "mpo", None),
        check_vma=False,
    )
```

profile of v0, /device:TPU:0, one launch (start us, length us, event | category | flops | bytes accessed | tf_op | source)
XLA Modules:
  0.0 144.9 jit_solution(14078317793506280598)
XLA Ops:
  6.5 0.0 all-gather.2.cloned.1.call-start
  7.8 1.6 %fusion.10 = bf16[1,256,256]{2,1,0:T(8,128)(2,1)} fusion(bf16[1,256,256]{2,1,0:T(8,128)(2,1)} %param.7, s32[]{:T(128)} %bitcast.17, s32[]{:T(128)} %bitcast.15), kind=kLoop, calls=%fused_computation.12 | loop fusion | flops 262144 | bytes 262152 | tf_op jit(solution)/shard_map/jit(_where)/select_n | solution.py:17
  9.4 0.0 all-gather.2.cloned.1.call-update
  9.5 0.0 reduce-scatter.7.cloned.1.call-start
  9.5 0.7 compare_select_fusion
  10.2 0.7 compare_and_fusion
  10.8 23.7 %all-gather.2.cloned.1.call-done = bf16[8,256,256]{2,1,0:T(8,128)(2,1)} async-done(((bf16[1,256,256]{2,1,0:T(8,128)(2,1)}), bf16[8,256,256]{2,1,0:T(8,128)(2,1)}) %all-gather.2.cloned.1.call-update) | async-done | bytes 1048592 | tf_op jit(solution)/shard_map/all_gather | solution.py:18
  34.6 5.9 %gather_fusion = bf16[40,256,256]{2,1,0:T(8,128)(2,1)} fusion(bf16[8,256,256]{2,1,0:T(8,128)(2,1)} %all-gather.2.cloned.1.call-done, s32[1024]{0:T(1024)S(1)} %pad_clamp_fusion), kind=kCustom, calls=%fused_computation | custom fusion | bytes 10485920 | tf_op jit(solution)/shard_map/jit(_take)/gather | solution.py:21
  40.5 5.8 %fusion.5 = bf16[40,256,256]{1,2,0:T(8,128)(2,1)S(1)} fusion(bf16[40,256,256]{2,1,0:T(8,128)(2,1)} %param.10, bf16[40,256,256]{2,1,0:T(8,128)(2,1)} %gather_fusion, pred[40]{0:T(512)(128)(4,1)S(1)} %compare_and_fusion), kind=kOutput, calls=%fused_computation.7 | convolution fusion | flops 1347420160 | bytes 15728680 | tf_op jit(solution)/shard_map/xvz,xzy->xvy/dot_general | solution.py:22
  46.3 0.0 slice-done
  46.3 0.0 slice-done.1
  46.4 0.0 copy-start.1
  46.4 5.6 %fusion = f32[40,4,64,256]{3,2,1,0:T(8,128)} fusion(bf16[40,4,64,256]{3,2,1,0:T(8,128)(2,1)S(1)} %bitcast.20, bf16[40,256,256]{2,1,0:T(8,128)(2,1)S(1)} %bitcast.19), kind=kOutput, calls=%fused_computation.2 | convolution fusion | flops 1342177280 | bytes 20971520 | tf_op jit(solution)/shard_map/tmrc,tdc->mtrd/dot_general | solution.py:26
  51.9 0.2 broadcast_in_dim.28
  52.2 0.0 copy-done.1
  52.2 14.8 %scatter_fusion = f32[4,8,64,256]{3,2,1,0:T(8,128)S(1)} fusion(f32[4,8,64,256]{3,2,1,0:T(8,128)S(1)} %broadcast_in_dim.28, s32[40]{0:T(128)S(1)} %copy-done.1, f32[40,4,64,256]{3,2,1,0:T(8,128)} %fusion), kind=kCustom, calls=%fused_computation.1 | custom fusion | flops 2621440 | bytes 31457440 | tf_op jit(solution)/shard_map/vmap()/scatter-add | solution.py:31
  67.0 0.0 copy-start
  67.0 1.3 copy-done
  68.4 0.0 reduce-scatter.7.cloned.1.call-update
  68.4 0.0 reduce-scatter.5.cloned.1.call-start
  68.4 34.8 %reduce-scatter.7.cloned.1.call-done = f32[1,8,64,256]{3,2,1,0:T(8,128)} async-done(((f32[4,8,64,256]{3,2,1,0:T(8,128)}), f32[1,8,64,256]{3,2,1,0:T(8,128)}) %reduce-scatter.7.cloned.1.call-update) | async-done | bytes 524304
  103.2 0.0 reduce-scatter.5.cloned.1.call-update
  103.3 33.5 %reduce-scatter.5.cloned.1.call-done = f32[1,64,256]{2,1,0:T(8,128)} async-done(((f32[8,64,256]{2,1,0:T(8,128)}), f32[1,64,256]{2,1,0:T(8,128)}) %reduce-scatter.5.cloned.1.call-update) | async-done | bytes 65552 | tf_op jit(solution)/shard_map/reduce_scatter | solution.py:35
  136.8 1.5 %select_convert_fusion = bf16[1,64,256]{2,1,0:T(8,128)(2,1)} fusion(f32[1,64,256]{2,1,0:T(8,128)} %reduce-scatter.5.cloned.1.call-done, s32[]{:T(128)} %bitcast.16, pred[64]{0:T(512)(128)(4,1)S(1)} %add_compare_fusion), kind=kLoop, calls=%fused_computation.13 | loop fusion | flops 49152 | bytes 98372 | tf_op jit(solution)/shard_map/convert_element_type | solution.py:42
  (5 shorter events, 0.0 us)
Async XLA Ops:
  6.5 28.0 %all-gather.2.cloned.1.call-start = ((), (), s32[]{:S(2)}) async-start(), calls=%async_computation.2 | async-start | bytes 1179648 | tf_op jit(solution)/shard_map/all_gather | solution.py:18
  9.5 93.8 %reduce-scatter.7.cloned.1.call-start = ((), (), s32[]{:S(2)}) async-start(), calls=%async_computation.4 | async-start | bytes 2621440
  34.6 11.8 %slice-start = ((s8[5242880]{0:T(1024)(128)(4,1)}), s8[1048576]{0:T(1024)(128)(4,1)S(1)}, s32[]{:S(2)}) async-start(s8[5242880]{0:T(1024)(128)(4,1)} %bitcast.18), calls=%async_computation.5 | async-start | bytes 2097152
  40.5 5.9 %slice-start.1 = ((s8[5242880]{0:T(1024)(128)(4,1)}), s8[4194304]{0:T(1024)(128)(4,1)S(1)}, s32[]{:S(2)}) async-start(s8[5242880]{0:T(1024)(128)(4,1)} %bitcast.18), calls=%async_computation.6 | async-start | bytes 8388608
  46.4 5.8 %copy-start.1 = (s32[40]{0:T(128)S(1)}, s32[40]{0:T(128)}, u32[]{:S(2)}) copy-start(s32[40]{0:T(128)} %param.12) | copy-start | bytes 484
  67.0 1.4 copy-start
  68.4 68.4 %reduce-scatter.5.cloned.1.call-start = ((), (), s32[]{:S(2)}) async-start(), calls=%async_computation.3 | async-start | bytes 589824 | tf_op jit(solution)/shard_map/reduce_scatter | solution.py:35
Sparse Core Ops, SparseCore 0:
  9.6 24.9 all-gather.1
  68.5 34.6 reduce-scatter.6
  105.5 31.2 reduce-scatter.4
where the time goes:
time: 145 us
  waiting for transfers between devices  92.1 us (64%)
  other arithmetic  19.3 us (13%)
  between operations  14.5 us (10%)
  matrix products  11.4 us (8%)
  local copies, waits for them, and re-layouts  7.48 us (5%)
    unnamed x4, waiting for transfers between devices  34.9 us
    reduce_scatter x1, waiting for transfers between devices, on_device(): lax.psum_scatter(row_sums[0], 'sec', scatter_dimension=0, tiled=True)  33.5 us
    all_gather x1, waiting for transfers between devices, on_device(): blocks = lax.all_gather(masked, 'sec', axis=0, tiled=True)  23.7 us
    scatter-add x1, other arithmetic, sector_sums(): return jax.ops.segment_sum(terms, task_out, num_segments=sectors)  14.8 us
    gather x1, local copies, waits for them, and re-layouts, on_device(): picked_tasks = jnp.take(blocks, task_in, axis=0)  5.89 us
    dot_general x1, matrix products, on_device(): jnp.einsum('xvz,xzy->xvy', left_environment_block, picked_tasks, preferre...  5.85 us
    dot_general x1, matrix products, on_device(): jnp.einsum('tmrc,tdc->mtrd', middle_split, right_env, preferred_element_t...  5.56 us
  transfers between devices with their start and end apart: 3, of which 3 were waited for; matrix products, arithmetic and copies ran while one was open for 1% of the time, Pallas kernels for 0%

commit v1 on v0

v1 whole, which is shorter than its diff:
```python
import functools

import jax
import jax.numpy as jnp
from jax import lax
from jax.experimental import pallas as pl
from jax.experimental.pallas import tpu as pltpu
from jax.sharding import PartitionSpec as P

CORES = 2
GROUP = 4


def live(shape, row0, rows, cols):
    row_ids = lax.broadcasted_iota(jnp.int32, shape, 0) + row0
    col_ids = lax.broadcasted_iota(jnp.int32, shape, 1)
    return (row_ids < rows) & (col_ids < cols)


def kernel(
    groups, chips, wave, ldim, rdim, tout, tin, left_hbm, right_hbm, out,
    blk, left, right, mids, cum, held, prev, last,
    sbuf0, rbuf0, acc1, sbuf1, rbuf1, sbuf2, rbuf2,
    load_sem, zs, zr, ps, pr, xs, xr, s0, r0, s1, r1, s2, r2,
):
    m = lax.axis_index("mpo")
    s = lax.axis_index("sec")
    z, c = s // CORES, s % CORES
    mate = z * CORES + 1 - c
    size = wave.shape[1]
    quarter = size // groups
    tasks = left.shape[0]
    sectors = chips * CORES

    def rows_of(g):
        return pl.ds(pl.multiple_of(g * quarter, quarter), quarter)

    def remote(src, dst, ssem, rsem, dev):
        return pltpu.make_async_remote_copy(
            src_ref=src, dst_ref=dst, send_sem=ssem, recv_sem=rsem,
            device_id=dev, device_id_type=pl.DeviceIdType.MESH,
        )

    loads = [
        pltpu.make_async_copy(left_hbm, left, load_sem.at[0]),
        pltpu.make_async_copy(right_hbm, right, load_sem.at[1]),
    ]
    for copy in loads:
        copy.start()
    barrier = pltpu.get_barrier_semaphore()
    mpo_peers = [lax.rem(m + j, groups) for j in range(1, groups)]
    chip_peers = [lax.rem(z + k, chips) for k in range(1, chips)]
    chip_from = [lax.rem(z + chips - k, chips) for k in range(1, chips)]
    peers = [(m, mate)] + [(g, s) for g in mpo_peers] + [(m, p * CORES + c) for p in chip_peers]
    for dev in peers:
        pl.semaphore_signal(barrier, inc=1, device_id=dev, device_id_type=pl.DeviceIdType.MESH)
    rows, cols = ldim[0], rdim[0]
    blk[s] = jnp.where(live((size, size), 0, rows, cols), wave[0], jnp.zeros_like(wave[0]))
    pl.semaphore_wait(barrier, len(peers))

    sends = []

    def go(copy):
        copy.start()
        sends.append(copy)
        return copy

    z_copies = []
    for k, p in enumerate(chip_peers):
        part = blk.at[s, rows_of(m)]
        z_copies.append(go(remote(part, part, zs.at[k], zr.at[k], (m, p * CORES + c))))
    p_copies = [go(remote(blk.at[s], blk.at[s], ps.at[0], pr.at[0], (m, mate)))]

    def clear(q, _):
        last[q] = 0
        return 0

    lax.fori_loop(0, sectors, clear, 0)

    def link(t, _):
        o = tout[t]

        def look(q, found):
            seen = last[q]
            hit = o == q
            last[q] = jnp.where(hit, t + 1, seen)
            return jnp.where(hit, seen, found)

        prev[t] = lax.fori_loop(0, sectors, look, 0, unroll=8)
        return 0

    lax.fori_loop(0, tasks, link, 0)
    cum[0] = jnp.zeros_like(cum[0])

    x_copies = []
    for k in range(chips - 1):
        z_copies[k].wait_recv()
        part = blk.at[chip_from[k] * CORES + c, rows_of(m)]
        x_copies.append([
            go(remote(part, part, xs.at[k, j], xr.at[k, j], (g, s)))
            for j, g in enumerate(mpo_peers)
        ])
    for k in range(chips - 1):
        for copy in x_copies[k]:
            copy.wait_recv()
        whole = blk.at[chip_from[k] * CORES + c]
        p_copies.append(go(remote(whole, whole, ps.at[k + 1], pr.at[k + 1], (m, mate))))
    for copy in loads:
        copy.wait()
    for copy in p_copies:
        copy.wait_recv()

    def first(i, _):
        for u in range(GROUP):
            t = i * GROUP + u
            mids[t] = jnp.dot(
                left[t], blk[tin[t]], preferred_element_type=jnp.float32
            ).astype(jnp.bfloat16)
        return 0

    lax.fori_loop(0, tasks // GROUP, first, 0)

    def second(i, _):
        for u in range(GROUP):
            t = i * GROUP + u
            product = lax.dot_general(
                mids[t], right[t], (((1,), (1,)), ((), ())), preferred_element_type=jnp.float32
            )
            cum[t + 1] = cum[prev[t]] + product
        return 0

    lax.fori_loop(0, tasks // GROUP, second, 0)

    order = chip_peers + [z]
    r0_copies = []
    for i, p in enumerate(order):
        sbuf0[i] = cum[last[p * CORES + 1 - c]].astype(jnp.bfloat16)
        r0_copies.append(go(remote(sbuf0.at[i], rbuf0.at[i], s0.at[i], r0.at[i], (m, mate))))
    r1_copies = []
    for i, p in enumerate(order):
        r0_copies[i].wait_recv()
        total = cum[last[p * CORES + c]] + rbuf0[i].astype(jnp.float32)
        held[...] = total
        sbuf1[i] = total.astype(jnp.bfloat16)
        r1_copies.append([
            go(remote(sbuf1.at[i, rows_of(g)], rbuf1.at[i, j], s1.at[i, j], r1.at[i, j], (g, s)))
            for j, g in enumerate(mpo_peers)
        ])
        acc1[i] = held[rows_of(m), :]
    r2_copies = []
    for i, p in enumerate(order):
        total = acc1[i]
        for j in range(groups - 1):
            r1_copies[i][j].wait_recv()
            total = total + rbuf1[i, j].astype(jnp.float32)
        if i < chips - 1:
            sbuf2[i] = total.astype(jnp.bfloat16)
            r2_copies.append(
                go(remote(sbuf2.at[i], rbuf2.at[i], s2.at[i], r2.at[i], (m, p * CORES + c)))
            )
    for k in range(chips - 1):
        r2_copies[k].wait_recv()
        total = total + rbuf2[k].astype(jnp.float32)
    keep = live(total.shape, m * quarter, rows, cols)
    out[0] = jnp.where(keep, total, jnp.zeros_like(total)).astype(jnp.bfloat16)
    for copy in sends:
        copy.wait_send()


def on_device(
    wavefunction, left_dims, right_dims, left_environment_block, right_env, task_out, task_in
):
    groups, sec = lax.axis_size("mpo"), lax.axis_size("sec")
    chips = sec // CORES
    _, size, width = wavefunction.shape
    quarter = size // groups
    tasks = task_out.shape[0]
    bf16, f32 = jnp.bfloat16, jnp.float32
    smem = pl.BlockSpec(memory_space=pltpu.SMEM)
    vmem = pl.BlockSpec(memory_space=pltpu.VMEM)
    dma = pltpu.SemaphoreType.DMA
    near, far = max(groups - 1, 1), max(chips - 1, 1)
    return pl.pallas_call(
        functools.partial(kernel, groups, chips),
        out_shape=jax.ShapeDtypeStruct((1, quarter, width), bf16),
        in_specs=[vmem, smem, smem, smem, smem]
        + [pl.BlockSpec(memory_space=pl.ANY)] * 2,
        out_specs=vmem,
        scratch_shapes=[
            pltpu.VMEM((sec, size, width), bf16),
            pltpu.VMEM((tasks, size, size), bf16),
            pltpu.VMEM((tasks, size, size), bf16),
            pltpu.VMEM((tasks, size, width), bf16),
            pltpu.VMEM((tasks + 1, size, width), f32),
            pltpu.VMEM((size, width), f32),
            pltpu.SMEM((tasks,), jnp.int32),
            pltpu.SMEM((sec,), jnp.int32),
            pltpu.VMEM((chips, size, width), bf16),
            pltpu.VMEM((chips, size, width), bf16),
            pltpu.VMEM((chips, quarter, width), f32),
            pltpu.VMEM((chips, size, width), bf16),
            pltpu.VMEM((chips, near, quarter, width), bf16),
            pltpu.VMEM((far, quarter, width), bf16),
            pltpu.VMEM((far, quarter, width), bf16),
            dma((2,)),
            dma((far,)), dma((far,)),
            dma((chips,)), dma((chips,)),
            dma((far, near)), dma((far, near)),
            dma((chips,)), dma((chips,)),
            dma((chips, near)), dma((chips, near)),
            dma((far,)), dma((far,)),
        ],
        compiler_params=pltpu.CompilerParams(
            collective_id=0, has_side_effects=True, vmem_limit_bytes=60 * 1024 * 1024
        ),
        name="apply_blocks",
    )(wavefunction, left_dims, right_dims, task_out, task_in, left_environment_block, right_env)


def solution(mesh):
    return jax.shard_map(
        on_device,
        mesh=mesh,
        in_specs=(
            P("sec", None, None),
            P("sec"),
            P("sec"),
            P(("mpo", "sec"), None, None),
            P(("mpo", "sec"), None, None),
            P(("mpo", "sec")),
            P(("mpo", "sec")),
        ),
        out_specs=P("sec", "mpo", None),
        check_vma=False,
    )
```

time: 145 us -> 37.4 us (0.26)
  waiting for transfers between devices: 92.1 us -> 0 us
  Pallas kernels: 0 us -> 34.5 us
  other arithmetic: 19.3 us -> 0 us
  between operations: 14.5 us -> 1.3 us
  matrix products: 11.4 us -> 0 us
  local copies, waits for them, and re-layouts: 7.48 us -> 1.38 us
    unnamed x4 -> x0, waiting for transfers between devices: 34.9 us -> none
    pallas_call x0 -> x1, Pallas kernels: none -> 34.5 us  [on_device(): pl.pallas_call(functools.partial(kernel, groups, chips), out_shape=jax.Sh...]
    reduce_scatter x1 -> x0, waiting for transfers between devices: 33.5 us -> none  [on_device(): lax.psum_scatter(row_sums[0], 'sec', scatter_dimension=0, tiled=True)]
    all_gather x1 -> x0, waiting for transfers between devices: 23.7 us -> none  [on_device(): blocks = lax.all_gather(masked, 'sec', axis=0, tiled=True)]
    scatter-add x1 -> x0, other arithmetic: 14.8 us -> none  [sector_sums(): return jax.ops.segment_sum(terms, task_out, num_segments=sectors)]
    dot_general x2 -> x0, matrix products: 11.4 us -> none  [the longest x1 5.85 us: on_device(): jnp.einsum('xvz,xzy->xvy', left_environment_block, picked_tasks, preferre...]
    gather x1 -> x0, local copies, waits for them, and re-layouts: 5.89 us -> none  [on_device(): picked_tasks = jnp.take(blocks, task_in, axis=0)]
    select_n x2 -> x0, other arithmetic: 2.26 us -> none  [the longest x1 1.6 us: on_device(): masked = jnp.where(live_cells, wavefunction, jnp.zeros_like(wavefunction))]
  transfers between devices with their start and end apart: 3 -> 0, of which waited for: 3 -> 0; matrix products, arithmetic and copies ran while one was open for 1% -> 0% of each run, Pallas kernels for 0% -> 0%
where the time goes in v1:
time: 37.4 us; the launch traced here: 37.2 us
  Pallas kernels  34.5 us (92%)
  local copies, waits for them, and re-layouts  1.38 us (4%)
  between operations  1.3 us (3%)
    pallas_call x1, Pallas kernels, on_device(): pl.pallas_call(functools.partial(kernel, groups, chips), out_shape=jax.Sh...  34.5 us
    unnamed x1, local copies, waits for them, and re-layouts  1.38 us

profile of v1, /device:TPU:0, one launch (start us, length us, event | category | flops | bytes accessed | tf_op | source)
XLA Modules:
  0.0 37.2 jit_solution(18444589564396090393)
XLA Ops:
  1.3 34.5 %apply_blocks.1 = bf16[1,64,256]{2,1,0:T(8,128)(2,1)} custom-call(bf16[1,256,256]{2,1,0:T(8,128)(2,1)} %wave.1, s32[1]{0:T(128)S(6)} %copy.9.ldim, s32[1]{0:T(128)S(6)} %copy.10.rdim, s32[40]{0:T(128)} %tout.1, s32[40]{0:T(128)} %tin.1, bf16[40,256,256]{2,1,0:T(8,128)(2,1)} %left_hbm.1, bf16[40,256,256]{2,1,0:T(8,128)(2,1)} %right_hbm.1), custom_call_target="tpu_custom_call" | custom-call | tf_op jit(solution)/shard_map/apply_blocks/pallas_call | solution.py:183
  35.8 1.4 %copy.11 = bf16[1,64,256]{2,1,0:T(8,128)(2,1)} copy(bf16[1,64,256]{2,1,0:T(8,128)(2,1)} %apply_blocks.1) | data formatting | bytes 65536

commit v2 on v1

--- a/solution.py
+++ b/solution.py
@@ -8,7 +8,7 @@
 from jax.sharding import PartitionSpec as P
 
 CORES = 2
-GROUP = 4
+GROUP = 20
 
 
 def live(shape, row0, rows, cols):
@@ -18,8 +18,8 @@
 
 
 def kernel(
-    groups, chips, wave, ldim, rdim, tout, tin, left_hbm, right_hbm, out,
-    blk, left, right, mids, cum, held, prev, last,
+    groups, chips, wave, ldim_hbm, rdim_hbm, tout, tin, left_hbm, right_hbm, out,
+    blk, left, right, mids, cum, held, prev, last, ldim, rdim,
     sbuf0, rbuf0, acc1, sbuf1, rbuf1, sbuf2, rbuf2,
     load_sem, zs, zr, ps, pr, xs, xr, s0, r0, s1, r1, s2, r2,
 ):
@@ -45,7 +45,11 @@
         pltpu.make_async_copy(left_hbm, left, load_sem.at[0]),
         pltpu.make_async_copy(right_hbm, right, load_sem.at[1]),
     ]
-    for copy in loads:
+    dims = [
+        pltpu.make_async_copy(ldim_hbm, ldim, load_sem.at[2]),
+        pltpu.make_async_copy(rdim_hbm, rdim, load_sem.at[3]),
+    ]
+    for copy in dims + loads:
         copy.start()
     barrier = pltpu.get_barrier_semaphore()
     mpo_peers = [lax.rem(m + j, groups) for j in range(1, groups)]
@@ -54,6 +58,8 @@
     peers = [(m, mate)] + [(g, s) for g in mpo_peers] + [(m, p * CORES + c) for p in chip_peers]
     for dev in peers:
         pl.semaphore_signal(barrier, inc=1, device_id=dev, device_id_type=pl.DeviceIdType.MESH)
+    for copy in dims:
+        copy.wait()
     rows, cols = ldim[0], rdim[0]
     blk[s] = jnp.where(live((size, size), 0, rows, cols), wave[0], jnp.zeros_like(wave[0]))
     pl.semaphore_wait(barrier, len(peers))
@@ -177,14 +183,14 @@
     tasks = task_out.shape[0]
     bf16, f32 = jnp.bfloat16, jnp.float32
     smem = pl.BlockSpec(memory_space=pltpu.SMEM)
+    hbm = pl.BlockSpec(memory_space=pl.ANY)
     vmem = pl.BlockSpec(memory_space=pltpu.VMEM)
     dma = pltpu.SemaphoreType.DMA
     near, far = max(groups - 1, 1), max(chips - 1, 1)
     return pl.pallas_call(
         functools.partial(kernel, groups, chips),
         out_shape=jax.ShapeDtypeStruct((1, quarter, width), bf16),
-        in_specs=[vmem, smem, smem, smem, smem]
-        + [pl.BlockSpec(memory_space=pl.ANY)] * 2,
+        in_specs=[vmem, hbm, hbm, smem, smem, hbm, hbm],
         out_specs=vmem,
         scratch_shapes=[
             pltpu.VMEM((sec, size, width), bf16),
@@ -195,6 +201,8 @@
             pltpu.VMEM((size, width), f32),
             pltpu.SMEM((tasks,), jnp.int32),
             pltpu.SMEM((sec,), jnp.int32),
+            pltpu.SMEM((1,), jnp.int32),
+            pltpu.SMEM((1,), jnp.int32),
             pltpu.VMEM((chips, size, width), bf16),
             pltpu.VMEM((chips, size, width), bf16),
             pltpu.VMEM((chips, quarter, width), f32),
@@ -202,7 +210,7 @@
             pltpu.VMEM((chips, near, quarter, width), bf16),
             pltpu.VMEM((far, quarter, width), bf16),
             pltpu.VMEM((far, quarter, width), bf16),
-            dma((2,)),
+            dma((4,)),
             dma((far,)), dma((far,)),
             dma((chips,)), dma((chips,)),
             dma((far, near)), dma((far, near)),

time: 37.4 us -> 34.7 us (0.928)
  Pallas kernels: 34.5 us -> 31.8 us
    pallas_call x1, Pallas kernels: 34.5 us -> 31.8 us  [on_device(): pl.pallas_call(functools.partial(kernel, groups, chips), out_shape=jax.Sh...]
where the time goes in v2:
time: 34.7 us; the launch traced here: 34.5 us
  Pallas kernels  31.8 us (92%)
  local copies, waits for them, and re-layouts  1.38 us (4%)
  between operations  1.3 us (4%)
    pallas_call x1, Pallas kernels, on_device(): pl.pallas_call(functools.partial(kernel, groups, chips), out_shape=jax.Sh...  31.8 us
    unnamed x1, local copies, waits for them, and re-layouts  1.38 us

profile of v2, /device:TPU:0, one launch (start us, length us, event | category | flops | bytes accessed | tf_op | source)
XLA Modules:
  0.0 34.5 jit_solution(9890554204272222593)
XLA Ops:
  1.3 31.8 %apply_blocks.1 = bf16[1,64,256]{2,1,0:T(8,128)(2,1)} custom-call(bf16[1,256,256]{2,1,0:T(8,128)(2,1)} %wave.1, s32[1]{0:T(128)S(6)} %copy.9.ldim_hbm, s32[1]{0:T(128)S(6)} %copy.10.rdim_hbm, s32[40]{0:T(128)} %tout.1, s32[40]{0:T(128)} %tin.1, bf16[40,256,256]{2,1,0:T(8,128)(2,1)} %left_hbm.1, bf16[40,256,256]{2,1,0:T(8,128)(2,1)} %right_hbm.1), custom_call_target="tpu_custom_call" | custom-call | tf_op jit(solution)/shard_map/apply_blocks/pallas_call | solution.py:190
  33.1 1.4 %copy.11 = bf16[1,64,256]{2,1,0:T(8,128)(2,1)} copy(bf16[1,64,256]{2,1,0:T(8,128)(2,1)} %apply_blocks.1) | data formatting | bytes 65536

commit v3 on v2

--- a/solution.py
+++ b/solution.py
@@ -116,26 +116,20 @@
     for copy in p_copies:
         copy.wait_recv()
 
-    def first(i, _):
-        for u in range(GROUP):
-            t = i * GROUP + u
+    def multiply(i, _):
+        group = [i * GROUP + u for u in range(GROUP)]
+        for t in group:
             mids[t] = jnp.dot(
                 left[t], blk[tin[t]], preferred_element_type=jnp.float32
             ).astype(jnp.bfloat16)
-        return 0
-
-    lax.fori_loop(0, tasks // GROUP, first, 0)
-
-    def second(i, _):
-        for u in range(GROUP):
-            t = i * GROUP + u
+        for t in group:
             product = lax.dot_general(
                 mids[t], right[t], (((1,), (1,)), ((), ())), preferred_element_type=jnp.float32
             )
             cum[t + 1] = cum[prev[t]] + product
         return 0
 
-    lax.fori_loop(0, tasks // GROUP, second, 0)
+    lax.fori_loop(0, tasks // GROUP, multiply, 0)
 
     order = chip_peers + [z]
     r0_copies = []

time: 34.7 us -> 34.3 us (0.988)
  Pallas kernels: 31.8 us -> 31.4 us
    pallas_call x1, Pallas kernels: 31.8 us -> 31.4 us  [on_device(): pl.pallas_call(functools.partial(kernel, groups, chips), out_shape=jax.Sh...]
where the time goes in v3:
time: 34.3 us; the launch traced here: 34.1 us
  Pallas kernels  31.4 us (92%)
  local copies, waits for them, and re-layouts  1.38 us (4%)
  between operations  1.3 us (4%)
    pallas_call x1, Pallas kernels, on_device(): pl.pallas_call(functools.partial(kernel, groups, chips), out_shape=jax.Sh...  31.4 us
    unnamed x1, local copies, waits for them, and re-layouts  1.38 us

profile of v3, /device:TPU:0, one launch (start us, length us, event | category | flops | bytes accessed | tf_op | source)
XLA Modules:
  0.0 34.1 jit_solution(6810670402385216193)
XLA Ops:
  1.3 31.4 %apply_blocks.1 = bf16[1,64,256]{2,1,0:T(8,128)(2,1)} custom-call(bf16[1,256,256]{2,1,0:T(8,128)(2,1)} %wave.1, s32[1]{0:T(128)S(6)} %copy.9.ldim_hbm, s32[1]{0:T(128)S(6)} %copy.10.rdim_hbm, s32[40]{0:T(128)} %tout.1, s32[40]{0:T(128)} %tin.1, bf16[40,256,256]{2,1,0:T(8,128)(2,1)} %left_hbm.1, bf16[40,256,256]{2,1,0:T(8,128)(2,1)} %right_hbm.1), custom_call_target="tpu_custom_call" | custom-call | tf_op jit(solution)/shard_map/apply_blocks/pallas_call | solution.py:184
  32.7 1.4 %copy.11 = bf16[1,64,256]{2,1,0:T(8,128)(2,1)} copy(bf16[1,64,256]{2,1,0:T(8,128)(2,1)} %apply_blocks.1) | data formatting | bytes 65536
